TPU v7x, 32 devices: a whole 2x2x4 slice. The times are simulated.
32 devices in a mesh: row: 4 (over y, x), col: 4 (over z), depth: 2 (over core).
Axes of the slice: x: 2, y: 2, z: 4, core: 2. Of those that a mesh axis runs over, the one named last changes fastest.
Arguments:
- orbitals: bfloat16 [2, 1024, 2, 4096], P(None, ('row', 'col'), 'depth'), may hold values from -20 to 20
- potential: float32 [2, 4096], P('depth'), may hold values from -6 to 6
Outputs:
- intersection: float32 [1024, 2, 1024], P(('row', 'depth'), None, 'col')
- applied: bfloat16 [2, 1024, 2, 4096], P(None, ('row', 'col'), 'depth')
All inputs are finite; a program needn't handle non-finite values.
Results may differ from a plain program's by a relative error of at most 0.001.
Values may be sent and summed in bfloat16 or wider, within the bound.
A program may use at most 128 MiB of HBM per device.

v0:
```python
import jax
import jax.numpy as jnp
from jax import lax
from jax.sharding import PartitionSpec as P

NX = 64


def with_halo(block, sides, width):
    for axis, dim in sides:
        count = lax.axis_size(axis)
        forward = [(i, i + 1) for i in range(count - 1)]
        forward.append((count - 1, 0))
        backward = [(target, source) for source, target in forward]
        low = lax.ppermute(
            lax.slice_in_dim(block, block.shape[dim] - width, None, axis=dim), axis, forward
        )
        high = lax.ppermute(lax.slice_in_dim(block, 0, width, axis=dim), axis, backward)
        block = jnp.concatenate([low, block, high], axis=dim)
    return block


def apply_operator(padded, potential):
    center = padded[:, :, 1:-1].astype(jnp.float32)
    below = padded[:, :, :-2].astype(jnp.float32)
    above = padded[:, :, 2:].astype(jnp.float32)
    flat_cells = center.shape[-1]
    xpos = jnp.arange(flat_cells) % NX
    yminus = jnp.roll(center, NX, axis=3)
    yplus = jnp.roll(center, -NX, axis=3)
    xminus = jnp.where(xpos == 0, jnp.roll(center, 1 - NX, axis=3), jnp.roll(center, 1, axis=3))
    xplus = jnp.where(
        xpos == NX - 1, jnp.roll(center, NX - 1, axis=3), jnp.roll(center, -1, axis=3)
    )
    lap = below + above + yminus + yplus + xminus + xplus - 6.0 * center
    return (-0.5 * lap + potential[None, None] * center).astype(jnp.bfloat16)


def contract(left, right):
    return lax.dot_general(
        left, right, (((1,), (1,)), ((), ())), preferred_element_type=jnp.float32
    )


def shards(orbitals, potential):
    parts, orbs, planes, cells = orbitals.shape
    flat = orbitals.reshape(parts, orbs, planes * cells)
    panel = lax.all_gather(flat, "col", axis=1, tiled=True)
    other = lax.all_gather(flat, "row", axis=1, tiled=True)
    padded = with_halo(orbitals, (("depth", 2),), 1)
    applied = apply_operator(padded, potential)
    dvol = 1.0 / (planes * lax.axis_size("depth") * cells)
    tile_cols = other.shape[1]
    real_rows = panel[0]
    imag_rows = panel[1]
    sreal = contract(real_rows, other[0]) + contract(imag_rows, other[1])
    simag = contract(real_rows, other[1]) - contract(imag_rows, other[0])
    summed = lax.psum_scatter(
        dvol * jnp.concatenate([sreal, simag], axis=1), "depth", scatter_dimension=0, tiled=True
    )
    intersection = summed.reshape(summed.shape[0], 2, tile_cols)
    intersection = lax.all_to_all(intersection, "col", split_axis=2, concat_axis=2, tiled=True)
    return (intersection, applied)


def solution(mesh):
    in_specs = (P(None, ("row", "col"), "depth", None), P("depth", None))
    out_specs = (P(("row", "depth"), None, "col"), P(None, ("row", "col"), "depth", None))
    return jax.shard_map(shards, mesh=mesh, in_specs=in_specs, out_specs=out_specs, check_vma=False)
```

profile of v0, /device:TPU:7, one launch (start us, length us, event | category | flops | bytes accessed | tf_op | source)
XLA Modules:
  0.0 182.7 jit_solution(16060242905263434024)
XLA Ops:
  7.2 0.0 copy-start
  7.2 0.0 all-gather.7.cloned.1.call-start
  7.2 0.7 all-gather.7.cloned.1.call-update
  7.9 0.0 all-gather.5.cloned.1.call-start
  8.0 0.7 all-gather.5.cloned.1.call-update
  8.7 0.0 reduce-scatter.2.cloned.1.call-start
  8.7 0.0 copy-done
  8.7 0.7 collective-permute-start
  9.5 0.1 collective-permute-start.1
  9.5 0.1 fusion.23
  9.6 0.7 fusion.20
  10.3 0.7 fusion.19
  11.0 1.8 fusion.21
  12.8 2.4 %fusion.22 = (f32[2,64,1,4032]{3,1,2,0:T(8,128)}, f32[2,64,1,4032]{3,1,2,0:T(8,128)}) fusion(bf16[2,64,1,4096]{3,1,2,0:T(8,128)(2,1)S(1)} %copy-done), kind=kLoop, calls=%fused_computation.32 | loop fusion | bytes 8257536 | tf_op jit(solution)/shard_map/jit(_roll_static)/slice | solution.py:30
  15.3 47.2 %all-gather.7.cloned.1.call-done = bf16[2,256,1,4096]{3,1,2,0:T(8,128)(2,1)} async-done(((bf16[2,64,1,4096]{3,1,2,0:T(8,128)(2,1)}), bf16[2,256,1,4096]{3,1,2,0:T(8,128)(2,1)}) %all-gather.7.cloned.1.call-update) | async-done | bytes 4194320 | tf_op jit(solution)/shard_map/all_gather | solution.py:49
  62.5 83.3 %all-gather.5.cloned.1.call-done = bf16[2,256,1,4096]{3,1,2,0:T(8,128)(2,1)} async-done(((bf16[2,64,1,4096]{3,1,2,0:T(8,128)(2,1)}), bf16[2,256,1,4096]{3,1,2,0:T(8,128)(2,1)}) %all-gather.5.cloned.1.call-update) | async-done | bytes 4194320 | tf_op jit(solution)/shard_map/all_gather | solution.py:48
  145.8 0.0 copy-start.2
  145.8 3.1 %fusion.7 = f32[256,256]{0,1:T(8,128)S(1)} fusion(bf16[2,256,1,4096]{3,1,2,0:T(8,128)(2,1)} %all-gather.5.cloned.1.call-done, bf16[2,256,1,4096]{3,1,2,0:T(8,128)(2,1)} %all-gather.7.cloned.1.call-done), kind=kOutput, calls=%fused_computation.14 | convolution fusion | flops 536870912 | bytes 4456448 | tf_op jit(solution)/shard_map/dot_general | solution.py:40
  148.9 0.3 copy-done.2
  149.3 0.0 copy-start.3
  149.3 2.5 %fusion.8 = f32[256,256]{0,1:T(8,128)S(1)} fusion(bf16[2,256,1,4096]{3,1,2,0:T(8,128)(2,1)} %all-gather.5.cloned.1.call-done, bf16[2,256,1,4096]{3,1,2,0:T(8,128)(2,1)S(1)} %copy-done.2), kind=kOutput, calls=%fused_computation.15 | convolution fusion | flops 536870912 | bytes 4456448 | tf_op jit(solution)/shard_map/dot_general | solution.py:40
  151.8 0.3 copy-done.3
  152.1 0.7 fusion.12
  152.8 0.7 fusion.11
  153.6 0.8 maximum_multiply_fusion
  154.4 0.0 reduce-scatter.2.cloned.1.call-update
  154.4 0.6 fusion.15
  155.0 0.0 copy-start.1
  155.0 2.4 %fusion.18 = (f32[2,64,1,4095]{3,1,2,0:T(8,128)}, f32[2,64,1,4095]{3,1,2,0:T(8,128)}) fusion(bf16[2,64,1,4096]{3,1,2,0:T(8,128)(2,1)S(1)} %copy-done), kind=kLoop, calls=%fused_computation.28 | loop fusion | bytes 8386560 | tf_op jit(solution)/shard_map/jit(_roll_static)/slice | solution.py:33
  157.5 4.4 %reduce-scatter.2.cloned.1.call-done = f32[128,512]{0,1:T(8,128)} async-done(((f32[256,512]{0,1:T(8,128)}), f32[128,512]{0,1:T(8,128)}) %reduce-scatter.2.cloned.1.call-update) | async-done | bytes 262160 | tf_op jit(solution)/shard_map/reduce_scatter | solution.py:58
  161.9 1.9 %copy.7 = f32[128,2,256]{0,1,2:T(2,128)} copy(f32[128,2,256]{0,2,1:T(8,128)} %bitcast.26) | data formatting | bytes 524288 | tf_op jit(solution)/shard_map/reshape | solution.py:61
  163.7 4.3 %all-to-all-start = ((f32[128,2,256]{0,1,2:T(2,128)}), f32[128,2,256]{0,1,2:T(2,128)S(1)}, u32[]{:S(2)}, u32[]{:S(2)}) async-start(f32[128,2,256]{0,1,2:T(2,128)} %copy.7), calls=%async_computation.1 | async-start | bytes 524288 | tf_op jit(solution)/shard_map/all_to_all | solution.py:62
  168.0 0.0 collective-permute-done
  168.0 0.0 collective-permute-done.1
  168.0 0.0 copy-done.1
  168.0 6.8 %fusion.6 = bf16[2,64,1,4096]{3,1,2,0:T(8,128)(2,1)} fusion(f32[2,64,1,4032]{3,1,2,0:T(8,128)} %get-tuple-element.15, f32[2,64,1,64]{3,1,2,0:T(8,128)S(1)} %get-tuple-element.17, f32[2,64,1,64]{3,1,2,0:T(8,128)S(1)} %get-tuple-element.16, f32[2,64,1,4032]{3,1,2,0:T(8,128)} %get-tuple-element.14, f32[2,64,1,63]{3,1,2,0:T(8,128)} %get-tuple-element.11, ...), kind=kLoop, calls=%fused_computation.11 | loop fusion | flops 11534336 | bytes 16801792 | tf_op jit(solution)/shard_map/convert_element_type | solution.py:36
  174.9 0.5 all-to-all-done
  175.4 0.8 copy.8
Async XLA Ops:
  7.2 1.5 copy-start
  7.2 55.4 %all-gather.7.cloned.1.call-start = ((), (), s32[]{:S(2)}) async-start(), calls=%async_computation.4 | async-start | bytes 5242880 | tf_op jit(solution)/shard_map/all_gather | solution.py:49
  7.9 137.9 %all-gather.5.cloned.1.call-start = ((), (), s32[]{:S(2)}) async-start(), calls=%async_computation.3 | async-start | bytes 5242880 | tf_op jit(solution)/shard_map/all_gather | solution.py:48
  8.7 153.2 %reduce-scatter.2.cloned.1.call-start = ((), (), s32[]{:S(2)}) async-start(), calls=%async_computation.2 | async-start | bytes 786432 | tf_op jit(solution)/shard_map/reduce_scatter | solution.py:58
  8.7 159.3 %collective-permute-start = (bf16[2,64,1,4096]{3,1,2,0:T(8,128)(2,1)S(1)}, bf16[2,64,1,4096]{3,1,2,0:T(8,128)(2,1)}, u32[]{:S(2)}, u32[]{:S(2)}) collective-permute-start(bf16[2,64,1,4096]{3,1,2,0:T(8,128)(2,1)S(1)} %copy-done), channel_id=1, source_target_pairs={{0,1},{1,0},{2,3},{3,2},{4,5},{5,4},{6,7},{7,6},{8,9},{9,8},{10,11... | collective-permute-start | bytes 3145736 | tf_op jit(solution)/shard_map/ppermute | solution.py:15
  9.5 158.6 %collective-permute-start.1 = (bf16[2,64,1,4096]{3,1,2,0:T(8,128)(2,1)S(1)}, bf16[2,64,1,4096]{3,1,2,0:T(8,128)(2,1)}, u32[]{:S(2)}, u32[]{:S(2)}) collective-permute-start(bf16[2,64,1,4096]{3,1,2,0:T(8,128)(2,1)S(1)} %copy-done), channel_id=1, source_target_pairs={{1,0},{0,1},{3,2},{2,3},{5,4},{4,5},{7,6},{6,7},{9,8},{8,9},{11,10... | collective-permute-start | bytes 3145736 | tf_op jit(solution)/shard_map/ppermute | solution.py:18
  145.8 3.4 %copy-start.2 = (bf16[2,256,1,4096]{3,1,2,0:T(8,128)(2,1)S(1)}, bf16[2,256,1,4096]{3,1,2,0:T(8,128)(2,1)}, u32[]{:S(2)}) copy-start(bf16[2,256,1,4096]{3,1,2,0:T(8,128)(2,1)} %all-gather.7.cloned.1.call-done) | copy-start | bytes 12582916
  149.3 2.8 %copy-start.3 = (bf16[2,256,1,4096]{3,1,2,0:T(8,128)(2,1)S(1)}, bf16[2,256,1,4096]{3,1,2,0:T(8,128)(2,1)}, u32[]{:S(2)}) copy-start(bf16[2,256,1,4096]{3,1,2,0:T(8,128)(2,1)} %all-gather.5.cloned.1.call-done) | copy-start | bytes 12582916
  155.0 13.0 %copy-start.1 = (f32[1,4096]{1,0:T(1,128)S(1)}, f32[1,4096]{1,0:T(1,128)}, u32[]{:S(2)}) copy-start(f32[1,4096]{1,0:T(1,128)} %param.3) | copy-start | bytes 49156
  163.7 11.6 %all-to-all-start = ((f32[128,2,256]{0,1,2:T(2,128)}), f32[128,2,256]{0,1,2:T(2,128)S(1)}, u32[]{:S(2)}, u32[]{:S(2)}) async-start(f32[128,2,256]{0,1,2:T(2,128)} %copy.7), calls=%async_computation.1 | async-start | bytes 524288 | tf_op jit(solution)/shard_map/all_to_all | solution.py:62
Sparse Core Ops, SparseCore 0:
  9.8 52.6 all-gather.6
  64.1 81.6 all-gather.4
  154.6 7.2 reduce-scatter.1
where the time goes:
time: 186 us; the launch traced here: 183 us
  waiting for transfers between devices  137 us (74%)
  between operations  13.8 us (7%)
  local copies, waits for them, and re-layouts  11.5 us (6%)
  other arithmetic  8.25 us (4%)
  matrix products  7.07 us (4%)
  starting transfers between devices  5.23 us (3%)
    all_gather x1, waiting for transfers between devices, shards(): panel = lax.all_gather(flat, 'col', axis=1, tiled=True)  83.3 us
    all_gather x1, waiting for transfers between devices, shards(): other = lax.all_gather(flat, 'row', axis=1, tiled=True)  47.2 us
    dot_general x4, matrix products, contract(): lax.dot_general(left, right, (((1,), (1,)), ((), ())), preferred_element_...  7.07 us
    convert_element_type x1, other arithmetic, apply_operator(): return (-0.5 * lap + potential[None, None] * center).astype(jnp.bfloat16)  6.81 us
    reduce_scatter x1, waiting for transfers between devices, shards(): lax.psum_scatter(dvol * jnp.concatenate([sreal, simag], axis=1), 'depth',...  4.4 us
    all_to_all x1, starting transfers between devices, shards(): lax.all_to_all(intersection, 'col', split_axis=2, concat_axis=2, tiled=True)  4.3 us
  transfers between devices with their start and end apart: 6, of which 4 were waited for; matrix products, arithmetic and copies ran while one was open for 14% of the time, Pallas kernels for 0%

commit v1 on v0

--- a/solution.py
+++ b/solution.py
@@ -1,9 +1,14 @@
+import functools
+
 import jax
 import jax.numpy as jnp
 from jax import lax
+from jax.experimental import pallas as pl
+from jax.experimental.pallas import tpu as pltpu
 from jax.sharding import PartitionSpec as P
 
 NX = 64
+MESH = pl.DeviceIdType.MESH
 
 
 def with_halo(block, sides, width):
@@ -63,7 +68,189 @@
     return (intersection, applied)
 
 
+def flip(a, b):
+    low = lax.rem(lax.rem(a, 2) + lax.rem(b, 2), 2)
+    high = lax.rem(lax.div(a, 2) + lax.div(b, 2), 2)
+    return 2 * high + low
+
+
+def stencil(orb, halo, pot, out):
+    parts, orbs, cells = orb.shape
+    step = 16
+    xpos = lax.broadcasted_iota(jnp.int32, (step, cells), 1) % NX
+    first, last = xpos == 0, xpos == NX - 1
+
+    def body(i, carry):
+        part = lax.div(i, orbs // step)
+        rows = pl.ds(pl.multiple_of(lax.rem(i, orbs // step) * step, step), step)
+        center = orb[part, rows, :].astype(jnp.float32)
+        side = halo[part, rows, :].astype(jnp.float32)
+        right = pltpu.roll(center, 1, 1)
+        left = pltpu.roll(center, cells - 1, 1)
+        yminus = pltpu.roll(center, NX, 1)
+        yplus = pltpu.roll(center, cells - NX, 1)
+        xminus = jnp.where(first, pltpu.roll(right, cells - NX, 1), right)
+        xplus = jnp.where(last, pltpu.roll(left, NX, 1), left)
+        lap = side + side + yminus + yplus + xminus + xplus - 6.0 * center
+        out[part, rows, :] = (-0.5 * lap + pot[0:1, :] * center).astype(out.dtype)
+        return carry
+
+    lax.fori_loop(0, parts * (orbs // step), body, 0)
+
+
+def kernel(dvol, orb, pot, inter, applied, halo, panel, acc, give, take, land,
+           hs, hr, ls, zs, zr, xs, xr, ds, dr, gs, gr, rs, rr):
+    r, c, d = lax.axis_index("row"), lax.axis_index("col"), lax.axis_index("depth")
+    parts, orbs, cells = orb.shape
+    quarter = cells // 4
+    half = acc.shape[2]
+    peer = (r, c, 1 - d)
+    zdev = [None] + [(r, flip(c, k), d) for k in (1, 2, 3)]
+    xdev = [None] + [(flip(r, k), c, d) for k in (1, 2)]
+
+    barrier = pltpu.get_barrier_semaphore()
+    friends = [peer] + zdev[1:] + xdev[1:]
+    for dev in friends:
+        pl.semaphore_signal(barrier, inc=1, device_id=dev, device_id_type=MESH)
+    pl.semaphore_wait(barrier, len(friends))
+
+    def send(src, dst, ssem, rsem, dev):
+        return pltpu.make_async_remote_copy(
+            src_ref=src, dst_ref=dst, send_sem=ssem, recv_sem=rsem,
+            device_id=dev, device_id_type=MESH,
+        )
+
+    def lanes(k):
+        return pl.ds(pl.multiple_of(k * quarter, quarter), quarter)
+
+    def block(j, k):
+        return panel.at[j, :, pl.ds(pl.multiple_of(k * orbs, orbs), orbs), :]
+
+    zsend = {}
+    for k in (3, 2, 1):
+        zsend[k] = send(orb.at[:, :, lanes(flip(c, k))], block(0, c), zs.at[k], zr.at[k], zdev[k])
+        zsend[k].start()
+    xsend = {}
+    for j in (1, 2):
+        xsend[0, j] = send(orb.at[:, :, lanes(c)], block(j, c), xs.at[0, j], xr.at[0, j], xdev[j])
+        xsend[0, j].start()
+    edge = send(orb, halo, hs, hr, peer)
+    edge.start()
+    local = pltpu.make_async_copy(orb.at[:, :, lanes(c)], block(0, c), ls)
+    local.start()
+
+    edge.wait()
+    stencil(orb, halo, pot, applied)
+    local.wait()
+
+    for k in (1, 2, 3):
+        zsend[k].wait_recv()
+        for j in (1, 2):
+            xsend[k, j] = send(block(0, flip(c, k)), block(j, flip(c, k)),
+                               xs.at[k, j], xr.at[k, j], xdev[j])
+            xsend[k, j].start()
+
+    def tile(slot, jl, jr):
+        for part in (0, 1):
+            for mine in (0, 1):
+                at = d if mine else 1 - d
+                rows = pl.ds(pl.multiple_of(at * half, half), half)
+                a, b = panel[jl, 0, rows, :], panel[jl, 1, rows, :]
+                if part == 0:
+                    s = contract(a, panel[jr, 0]) + contract(b, panel[jr, 1])
+                else:
+                    s = contract(a, panel[jr, 1]) - contract(b, panel[jr, 0])
+                if mine:
+                    acc[slot, part] = s
+                else:
+                    give[slot, part] = s
+        cp = send(give.at[slot], take.at[slot], ds.at[slot], dr.at[slot], peer)
+        cp.start()
+        return cp
+
+    def ship(t):
+        to = flip(r, jnp.int32(t))
+        gap = flip(c, to)
+        return to, gap, send(acc.at[t], land.at[gap], gs.at[t], gr.at[gap], (r, to, d))
+
+    def start_ship(t):
+        to, gap, cp = ship(t)
+
+        @pl.when(to != c)
+        def _():
+            cp.start()
+
+    pair = {0: tile(0, 0, 0)}
+    for k in (0, 1, 2, 3):
+        xsend[k, 1].wait_recv()
+        xsend[k, 2].wait_recv()
+    pair[4] = tile(4, 1, 2)
+    pair[1] = tile(1, 0, 1)
+    pair[2] = tile(2, 0, 2)
+    pair[4].wait_recv()
+    acc[4] += take[4]
+    cross = send(acc.at[4], acc.at[3], rs, rr, xdev[1])
+    cross.start()
+    for t in (0, 1, 2):
+        pair[t].wait_recv()
+        acc[t] += take[t]
+        start_ship(t)
+    cross.wait_recv()
+    start_ship(3)
+
+    total = acc[flip(r, c)]
+    for k in (1, 2, 3):
+        send(acc.at[0], land.at[k], gs.at[0], gr.at[k], zdev[k]).wait_recv()
+        total = total + land[k]
+    inter[...] = total * dvol
+
+    for cp in [edge, cross] + list(pair.values()) + list(zsend.values()) + list(xsend.values()):
+        if cp is not edge:
+            cp.wait_send()
+    for t in (0, 1, 2, 3):
+        to, gap, cp = ship(t)
+
+        @pl.when(to != c)
+        def _():
+            cp.wait_send()
+
+
+def exchange(orbitals, potential):
+    parts, orbs, planes, cells = orbitals.shape
+    rows = orbs * lax.axis_size("col")
+    half = rows // 2
+    dvol = 1.0 / (planes * lax.axis_size("depth") * cells)
+    vmem = pl.BlockSpec(memory_space=pltpu.VMEM)
+    dma = pltpu.SemaphoreType.DMA
+    inter, applied = pl.pallas_call(
+        functools.partial(kernel, dvol),
+        out_shape=(
+            jax.ShapeDtypeStruct((2, half, rows), jnp.float32),
+            jax.ShapeDtypeStruct((parts, orbs, cells), jnp.bfloat16),
+        ),
+        in_specs=[vmem, vmem],
+        out_specs=(vmem, vmem),
+        scratch_shapes=[
+            pltpu.VMEM((parts, orbs, cells), jnp.bfloat16),
+            pltpu.VMEM((3, parts, rows, cells // 4), jnp.bfloat16),
+            pltpu.VMEM((5, 2, half, rows), jnp.float32),
+            pltpu.VMEM((5, 2, half, rows), jnp.float32),
+            pltpu.VMEM((5, 2, half, rows), jnp.float32),
+            pltpu.VMEM((4, 2, half, rows), jnp.float32),
+            dma, dma, dma, dma((4,)), dma((4,)), dma((4, 3)), dma((4, 3)),
+            dma((5,)), dma((5,)), dma((4,)), dma((4,)), dma, dma,
+        ],
+        compiler_params=pltpu.CompilerParams(
+            collective_id=0, has_side_effects=True, vmem_limit_bytes=60000000
+        ),
+        name="overlap",
+    )(orbitals.reshape(parts, orbs, cells), potential)
+    return jnp.transpose(inter, (1, 0, 2)), applied.reshape(orbitals.shape)
+
+
 def solution(mesh):
     in_specs = (P(None, ("row", "col"), "depth", None), P("depth", None))
     out_specs = (P(("row", "depth"), None, "col"), P(None, ("row", "col"), "depth", None))
-    return jax.shard_map(shards, mesh=mesh, in_specs=in_specs, out_specs=out_specs, check_vma=False)
+    sizes = tuple(mesh.shape[axis] for axis in ("row", "col", "depth"))
+    body = exchange if sizes == (4, 4, 2) else shards
+    return jax.shard_map(body, mesh=mesh, in_specs=in_specs, out_specs=out_specs, check_vma=False)

time: 186 us -> 76.7 us (0.41); the launches traced: 183 us -> 76.5 us
  waiting for transfers between devices: 137 us -> 0 us
  Pallas kernels: 0 us -> 71.7 us
  between operations: 13.8 us -> 0.64 us
  other arithmetic: 8.25 us -> 0 us
  local copies, waits for them, and re-layouts: 11.5 us -> 4.14 us
  matrix products: 7.07 us -> 0 us
  starting transfers between devices: 5.23 us -> 0 us
    all_gather x2 -> x0, waiting for transfers between devices: 131 us -> none  [the longest x1 83.3 us: shards(): panel = lax.all_gather(flat, 'col', axis=1, tiled=True)]
    pallas_call x0 -> x1, Pallas kernels: none -> 71.7 us  [exchange(): pl.pallas_call(functools.partial(kernel, dvol), out_shape=(jax.ShapeDtype...]
    slice x6 -> x0, local copies, waits for them, and re-layouts: 8.17 us -> none  [the longest x2 3.13 us: apply_operator(): jnp.roll(center, -1, axis=3)]
    dot_general x4 -> x0, matrix products: 7.07 us -> none  [contract(): lax.dot_general(left, right, (((1,), (1,)), ((), ())), preferred_element_...]
    convert_element_type x1 -> x0, other arithmetic: 6.81 us -> none  [apply_operator(): return (-0.5 * lap + potential[None, None] * center).astype(jnp.bfloat16)]
    reduce_scatter x1 -> x0, waiting for transfers between devices: 4.4 us -> none  [shards(): lax.psum_scatter(dvol * jnp.concatenate([sreal, simag], axis=1), 'depth',...]
    all_to_all x1 -> x0, starting transfers between devices: 4.3 us -> none  [shards(): lax.all_to_all(intersection, 'col', split_axis=2, concat_axis=2, tiled=True)]
    unnamed x9 -> x2, local copies, waits for them, and re-layouts: 1.51 us -> 4.14 us
  transfers between devices with their start and end apart: 6 -> 0, of which waited for: 4 -> 0; matrix products, arithmetic and copies ran while one was open for 14% -> 0% of each run, Pallas kernels for 0% -> 0%
where the time goes in v1:
time: 76.7 us; the launch traced here: 76.5 us
  Pallas kernels  71.7 us (93%)
  local copies, waits for them, and re-layouts  4.14 us (5%)
    pallas_call x1, Pallas kernels, exchange(): pl.pallas_call(functools.partial(kernel, dvol), out_shape=(jax.ShapeDtype...  71.7 us
    unnamed x2, local copies, waits for them, and re-layouts  4.14 us

profile of v1, /device:TPU:7, one launch (start us, length us, event | category | flops | bytes accessed | tf_op | source)
XLA Modules:
  0.0 76.5 jit_solution(18022936571108139220)
XLA Ops:
  0.6 71.7 %overlap.1 = (f32[2,128,256]{2,1,0:T(8,128)}, bf16[2,64,4096]{2,1,0:T(8,128)(2,1)}) custom-call(bf16[2,64,4096]{2,1,0:T(8,128)(2,1)} %bitcast.5, f32[1,4096]{1,0:T(1,128)} %pot.1), custom_call_target="tpu_custom_call" | custom-call | tf_op jit(solution)/shard_map/overlap/pallas_call | solution.py:225
  72.4 1.9 %copy.4 = f32[128,2,256]{2,1,0:T(2,128)} copy(f32[128,2,256]{2,0,1:T(8,128)} %bitcast.7) | data formatting | bytes 524288
  74.2 2.3 %copy.7 = bf16[2,64,1,4096]{3,1,2,0:T(8,128)(2,1)} copy(bf16[2,64,1,4096]{3,1,2,0:T(8,128)(2,1)} %bitcast.6) | data formatting | bytes 2097152

commit v2 on v1

--- a/solution.py
+++ b/solution.py
@@ -127,7 +127,7 @@
         return panel.at[j, :, pl.ds(pl.multiple_of(k * orbs, orbs), orbs), :]
 
     zsend = {}
-    for k in (3, 2, 1):
+    for k in (1, 3, 2):
         zsend[k] = send(orb.at[:, :, lanes(flip(c, k))], block(0, c), zs.at[k], zr.at[k], zdev[k])
         zsend[k].start()
     xsend = {}
@@ -143,7 +143,7 @@
     stencil(orb, halo, pot, applied)
     local.wait()
 
-    for k in (1, 2, 3):
+    for k in (1, 3, 2):
         zsend[k].wait_recv()
         for j in (1, 2):
             xsend[k, j] = send(block(0, flip(c, k)), block(j, flip(c, k)),
@@ -180,20 +180,24 @@
         def _():
             cp.start()
 
+    def settle(t):
+        pair[t].wait_recv()
+        acc[t] += take[t]
+
     pair = {0: tile(0, 0, 0)}
-    for k in (0, 1, 2, 3):
+    settle(0)
+    start_ship(0)
+    for k in (0, 1, 3, 2):
         xsend[k, 1].wait_recv()
         xsend[k, 2].wait_recv()
     pair[4] = tile(4, 1, 2)
     pair[1] = tile(1, 0, 1)
-    pair[2] = tile(2, 0, 2)
-    pair[4].wait_recv()
-    acc[4] += take[4]
+    settle(4)
     cross = send(acc.at[4], acc.at[3], rs, rr, xdev[1])
     cross.start()
-    for t in (0, 1, 2):
-        pair[t].wait_recv()
-        acc[t] += take[t]
+    pair[2] = tile(2, 0, 2)
+    for t in (1, 2):
+        settle(t)
         start_ship(t)
     cross.wait_recv()
     start_ship(3)
@@ -241,7 +245,7 @@
             dma((5,)), dma((5,)), dma((4,)), dma((4,)), dma, dma,
         ],
         compiler_params=pltpu.CompilerParams(
-            collective_id=0, has_side_effects=True, vmem_limit_bytes=60000000
+            collective_id=0, has_side_effects=True, vmem_limit_bytes=24000000
         ),
         name="overlap",
     )(orbitals.reshape(parts, orbs, cells), potential)

time: 76.7 us -> 67.3 us (0.88)
  Pallas kernels: 71.7 us -> 62.6 us
    pallas_call x1, Pallas kernels: 71.7 us -> 62.6 us  [exchange(): pl.pallas_call(functools.partial(kernel, dvol), out_shape=(jax.ShapeDtype...]
    unnamed x2 -> x6, local copies, waits for them, and re-layouts: 4.14 us -> 3.81 us
where the time goes in v2:
time: 67.3 us; the launch traced here: 67 us
  Pallas kernels  62.6 us (93%)
  local copies, waits for them, and re-layouts  3.81 us (6%)
    pallas_call x1, Pallas kernels, exchange(): pl.pallas_call(functools.partial(kernel, dvol), out_shape=(jax.ShapeDtype...  62.6 us
    unnamed x6, local copies, waits for them, and re-layouts  3.81 us

profile of v2, /device:TPU:7, one launch (start us, length us, event | category | flops | bytes accessed | tf_op | source)
XLA Modules:
  0.0 67.0 jit_solution(8728682590940202522)
XLA Ops:
  0.6 0.0 copy-start
  0.6 1.2 %copy-done = bf16[2,64,1,4096]{3,1,2,0:T(8,128)(2,1)S(1)} copy-done((bf16[2,64,1,4096]{3,1,2,0:T(8,128)(2,1)S(1)}, bf16[2,64,1,4096]{3,1,2,0:T(8,128)(2,1)}, u32[]{:S(2)}) %copy-start) | copy-done | bytes 1048600
  1.9 0.0 copy-start.1
  1.9 0.7 %copy-done.1 = f32[1,4096]{1,0:T(1,128)S(1)} copy-done((f32[1,4096]{1,0:T(1,128)S(1)}, f32[1,4096]{1,0:T(1,128)}, u32[]{:S(2)}) %copy-start.1) | copy-done | bytes 16408
  2.6 62.6 %overlap.1 = (f32[2,128,256]{2,1,0:T(8,128)S(1)}, bf16[2,64,4096]{2,1,0:T(8,128)(2,1)S(1)}) custom-call(bf16[2,64,4096]{2,1,0:T(8,128)(2,1)S(1)} %bitcast.5, f32[1,4096]{1,0:T(1,128)S(1)} %copy-done.1), custom_call_target="tpu_custom_call" | custom-call | tf_op jit(solution)/shard_map/overlap/pallas_call | solution.py:229
  65.1 0.9 %copy.4 = f32[128,2,256]{2,1,0:T(2,128)} copy(f32[128,2,256]{2,0,1:T(8,128)S(1)} %bitcast.7) | data formatting | bytes 524288
  66.0 1.0 %copy.7 = bf16[2,64,1,4096]{3,1,2,0:T(8,128)(2,1)} copy(bf16[2,64,1,4096]{3,1,2,0:T(8,128)(2,1)S(1)} %bitcast.6) | data formatting | bytes 2097152
Async XLA Ops:
  0.6 1.2 %copy-start = (bf16[2,64,1,4096]{3,1,2,0:T(8,128)(2,1)S(1)}, bf16[2,64,1,4096]{3,1,2,0:T(8,128)(2,1)}, u32[]{:S(2)}) copy-start(bf16[2,64,1,4096]{3,1,2,0:T(8,128)(2,1)} %param.2) | copy-start | bytes 3145732
  1.9 0.7 %copy-start.1 = (f32[1,4096]{1,0:T(1,128)S(1)}, f32[1,4096]{1,0:T(1,128)}, u32[]{:S(2)}) copy-start(f32[1,4096]{1,0:T(1,128)} %pot.1) | copy-start | bytes 49156

commit v3 on v2

--- a/solution.py
+++ b/solution.py
@@ -98,12 +98,16 @@
     lax.fori_loop(0, parts * (orbs // step), body, 0)
 
 
-def kernel(dvol, orb, pot, inter, applied, halo, panel, acc, give, take, land,
-           hs, hr, ls, zs, zr, xs, xr, ds, dr, gs, gr, rs, rr):
+def kernel(dvol, orb_hbm, pot_hbm, inter, applied, orb, pot, halo, panel, acc, give, take,
+           land, relay, ins, hs, hr, ls, zs, zr, xs, xr, ds, dr, gs, gr, qr, rs, rr):
     r, c, d = lax.axis_index("row"), lax.axis_index("col"), lax.axis_index("depth")
     parts, orbs, cells = orb.shape
     quarter = cells // 4
     half = acc.shape[2]
+    load = pltpu.make_async_copy(orb_hbm, orb, ins.at[0])
+    load.start()
+    load_pot = pltpu.make_async_copy(pot_hbm, pot, ins.at[1])
+    load_pot.start()
     peer = (r, c, 1 - d)
     zdev = [None] + [(r, flip(c, k), d) for k in (1, 2, 3)]
     xdev = [None] + [(flip(r, k), c, d) for k in (1, 2)]
@@ -112,6 +116,7 @@
     friends = [peer] + zdev[1:] + xdev[1:]
     for dev in friends:
         pl.semaphore_signal(barrier, inc=1, device_id=dev, device_id_type=MESH)
+    load.wait()
     pl.semaphore_wait(barrier, len(friends))
 
     def send(src, dst, ssem, rsem, dev):
@@ -123,62 +128,79 @@
     def lanes(k):
         return pl.ds(pl.multiple_of(k * quarter, quarter), quarter)
 
-    def block(j, k):
-        return panel.at[j, :, pl.ds(pl.multiple_of(k * orbs, orbs), orbs), :]
-
-    zsend = {}
+    def block(j, k, part):
+        return panel.at[j, part, pl.ds(pl.multiple_of(k * orbs, orbs), orbs), :]
+
+    zsend, xsend = {}, {}
     for k in (1, 3, 2):
-        zsend[k] = send(orb.at[:, :, lanes(flip(c, k))], block(0, c), zs.at[k], zr.at[k], zdev[k])
-        zsend[k].start()
-    xsend = {}
-    for j in (1, 2):
-        xsend[0, j] = send(orb.at[:, :, lanes(c)], block(j, c), xs.at[0, j], xr.at[0, j], xdev[j])
-        xsend[0, j].start()
+        for p in (0, 1):
+            zsend[k, p] = send(orb.at[p, :, lanes(flip(c, k))], block(0, c, p),
+                               zs.at[k, p], zr.at[k, p], zdev[k])
+            zsend[k, p].start()
+    for p in (0, 1):
+        for j in (1, 2):
+            xsend[0, j, p] = send(orb.at[p, :, lanes(c)], block(j, c, p),
+                                  xs.at[0, j, p], xr.at[0, j, p], xdev[j])
+            xsend[0, j, p].start()
     edge = send(orb, halo, hs, hr, peer)
     edge.start()
-    local = pltpu.make_async_copy(orb.at[:, :, lanes(c)], block(0, c), ls)
-    local.start()
-
+    local = [pltpu.make_async_copy(orb.at[p, :, lanes(c)], block(0, c, p), ls.at[p])
+             for p in (0, 1)]
+    for cp in local:
+        cp.start()
+
+    load_pot.wait()
     edge.wait()
     stencil(orb, halo, pot, applied)
-    local.wait()
+    for cp in local:
+        cp.wait()
 
     for k in (1, 3, 2):
-        zsend[k].wait_recv()
-        for j in (1, 2):
-            xsend[k, j] = send(block(0, flip(c, k)), block(j, flip(c, k)),
-                               xs.at[k, j], xr.at[k, j], xdev[j])
-            xsend[k, j].start()
+        for p in (0, 1):
+            zsend[k, p].wait_recv()
+            for j in (1, 2):
+                xsend[k, j, p] = send(block(0, flip(c, k), p), block(j, flip(c, k), p),
+                                      xs.at[k, j, p], xr.at[k, j, p], xdev[j])
+                xsend[k, j, p].start()
 
     def tile(slot, jl, jr):
+        a, b = panel[jl, 0], panel[jl, 1]
         for part in (0, 1):
-            for mine in (0, 1):
-                at = d if mine else 1 - d
-                rows = pl.ds(pl.multiple_of(at * half, half), half)
-                a, b = panel[jl, 0, rows, :], panel[jl, 1, rows, :]
-                if part == 0:
-                    s = contract(a, panel[jr, 0]) + contract(b, panel[jr, 1])
-                else:
-                    s = contract(a, panel[jr, 1]) - contract(b, panel[jr, 0])
-                if mine:
-                    acc[slot, part] = s
-                else:
-                    give[slot, part] = s
+            if part == 0:
+                s = contract(a, panel[jr, 0]) + contract(b, panel[jr, 1])
+            else:
+                s = contract(a, panel[jr, 1]) - contract(b, panel[jr, 0])
+            acc[slot, part] = jnp.where(d == 0, s[:half], s[half:])
+            give[slot, part] = jnp.where(d == 0, s[half:], s[:half])
         cp = send(give.at[slot], take.at[slot], ds.at[slot], dr.at[slot], peer)
         cp.start()
         return cp
 
+    inner = lax.rem(c + 1, 4) >= 2
+
     def ship(t):
         to = flip(r, jnp.int32(t))
-        gap = flip(c, to)
-        return to, gap, send(acc.at[t], land.at[gap], gs.at[t], gr.at[gap], (r, to, d))
+        return to, lax.div(to, 2) != lax.div(c, 2)
 
     def start_ship(t):
-        to, gap, cp = ship(t)
-
-        @pl.when(to != c)
-        def _():
-            cp.start()
+        to, across = ship(t)
+
+        @pl.when(jnp.logical_and(to != c, jnp.logical_not(across)))
+        def _():
+            send(acc.at[t], land.at[0], gs.at[t], gr.at[0], zdev[1]).start()
+
+        @pl.when(jnp.logical_and(across, jnp.logical_not(inner)))
+        def _():
+            send(acc.at[t], relay.at[t], gs.at[t], qr.at[t], zdev[1]).start()
+
+    def pass_on(t):
+        to, across = ship(t)
+
+        @pl.when(jnp.logical_and(across, inner))
+        def _():
+            send(acc.at[t], relay.at[t], gs.at[t], qr.at[t], zdev[1]).wait_recv()
+            acc[t] += relay[t]
+            send(acc.at[t], land.at[1], gs.at[t], gr.at[1], (r, to, d)).start()
 
     def settle(t):
         pair[t].wait_recv()
@@ -188,23 +210,29 @@
     settle(0)
     start_ship(0)
     for k in (0, 1, 3, 2):
-        xsend[k, 1].wait_recv()
-        xsend[k, 2].wait_recv()
+        for j in (1, 2):
+            for p in (0, 1):
+                xsend[k, j, p].wait_recv()
     pair[4] = tile(4, 1, 2)
     pair[1] = tile(1, 0, 1)
     settle(4)
     cross = send(acc.at[4], acc.at[3], rs, rr, xdev[1])
     cross.start()
+    settle(1)
+    start_ship(1)
     pair[2] = tile(2, 0, 2)
-    for t in (1, 2):
-        settle(t)
-        start_ship(t)
+    pass_on(0)
+    settle(2)
+    start_ship(2)
+    pass_on(1)
     cross.wait_recv()
     start_ship(3)
+    pass_on(2)
+    pass_on(3)
 
     total = acc[flip(r, c)]
-    for k in (1, 2, 3):
-        send(acc.at[0], land.at[k], gs.at[0], gr.at[k], zdev[k]).wait_recv()
+    for k in (0, 1):
+        send(acc.at[0], land.at[k], gs.at[0], gr.at[k], zdev[1]).wait_recv()
         total = total + land[k]
     inter[...] = total * dvol
 
@@ -212,11 +240,11 @@
         if cp is not edge:
             cp.wait_send()
     for t in (0, 1, 2, 3):
-        to, gap, cp = ship(t)
+        to, across = ship(t)
 
         @pl.when(to != c)
         def _():
-            cp.wait_send()
+            send(acc.at[t], land.at[0], gs.at[t], gr.at[0], zdev[1]).wait_send()
 
 
 def exchange(orbitals, potential):
@@ -232,17 +260,20 @@
             jax.ShapeDtypeStruct((2, half, rows), jnp.float32),
             jax.ShapeDtypeStruct((parts, orbs, cells), jnp.bfloat16),
         ),
-        in_specs=[vmem, vmem],
+        in_specs=[pl.BlockSpec(memory_space=pltpu.HBM)] * 2,
         out_specs=(vmem, vmem),
         scratch_shapes=[
+            pltpu.VMEM((parts, orbs, cells), jnp.bfloat16),
+            pltpu.VMEM(potential.shape, jnp.float32),
             pltpu.VMEM((parts, orbs, cells), jnp.bfloat16),
             pltpu.VMEM((3, parts, rows, cells // 4), jnp.bfloat16),
             pltpu.VMEM((5, 2, half, rows), jnp.float32),
             pltpu.VMEM((5, 2, half, rows), jnp.float32),
             pltpu.VMEM((5, 2, half, rows), jnp.float32),
+            pltpu.VMEM((2, 2, half, rows), jnp.float32),
             pltpu.VMEM((4, 2, half, rows), jnp.float32),
-            dma, dma, dma, dma((4,)), dma((4,)), dma((4, 3)), dma((4, 3)),
-            dma((5,)), dma((5,)), dma((4,)), dma((4,)), dma, dma,
+            dma((2,)), dma, dma, dma((2,)), dma((4, 2)), dma((4, 2)), dma((4, 3, 2)),
+            dma((4, 3, 2)), dma((5,)), dma((5,)), dma((4,)), dma((2,)), dma((4,)), dma, dma,
         ],
         compiler_params=pltpu.CompilerParams(
             collective_id=0, has_side_effects=True, vmem_limit_bytes=24000000

time: 67.3 us -> 66.8 us (level)
  no operation moved by 1% of the time
where the time goes in v3:
time: 66.8 us; the launch traced here: 66.6 us
  Pallas kernels  62.2 us (93%)
  local copies, waits for them, and re-layouts  3.81 us (6%)
    pallas_call x1, Pallas kernels, exchange(): pl.pallas_call(functools.partial(kernel, dvol), out_shape=(jax.ShapeDtype...  62.2 us
    unnamed x6, local copies, waits for them, and re-layouts  3.81 us

profile of v3, /device:TPU:7, one launch (start us, length us, event | category | flops | bytes accessed | tf_op | source)
XLA Modules:
  0.0 66.6 jit_solution(4039592432566962256)
XLA Ops:
  0.6 0.0 copy-start
  0.6 1.2 %copy-done = bf16[2,64,1,4096]{3,1,2,0:T(8,128)(2,1)S(1)} copy-done((bf16[2,64,1,4096]{3,1,2,0:T(8,128)(2,1)S(1)}, bf16[2,64,1,4096]{3,1,2,0:T(8,128)(2,1)}, u32[]{:S(2)}) %copy-start) | copy-done | bytes 1048600
  1.9 0.0 copy-start.1
  1.9 0.7 %copy-done.1 = f32[1,4096]{1,0:T(1,128)S(1)} copy-done((f32[1,4096]{1,0:T(1,128)S(1)}, f32[1,4096]{1,0:T(1,128)}, u32[]{:S(2)}) %copy-start.1) | copy-done | bytes 16408
  2.6 62.2 %overlap.1 = (f32[2,128,256]{2,1,0:T(8,128)S(1)}, bf16[2,64,4096]{2,1,0:T(8,128)(2,1)S(1)}) custom-call(bf16[2,64,4096]{2,1,0:T(8,128)(2,1)S(1)} %bitcast.5, f32[1,4096]{1,0:T(1,128)S(1)} %copy-done.1), custom_call_target="tpu_custom_call" | custom-call | tf_op jit(solution)/shard_map/overlap/pallas_call | solution.py:257
  64.7 0.9 %copy.4 = f32[128,2,256]{2,1,0:T(2,128)} copy(f32[128,2,256]{2,0,1:T(8,128)S(1)} %bitcast.7) | data formatting | bytes 524288
  65.6 1.0 %copy.7 = bf16[2,64,1,4096]{3,1,2,0:T(8,128)(2,1)} copy(bf16[2,64,1,4096]{3,1,2,0:T(8,128)(2,1)S(1)} %bitcast.6) | data formatting | bytes 2097152
Async XLA Ops:
  0.6 1.2 %copy-start = (bf16[2,64,1,4096]{3,1,2,0:T(8,128)(2,1)S(1)}, bf16[2,64,1,4096]{3,1,2,0:T(8,128)(2,1)}, u32[]{:S(2)}) copy-start(bf16[2,64,1,4096]{3,1,2,0:T(8,128)(2,1)} %param.2) | copy-start | bytes 3145732
  1.9 0.7 %copy-start.1 = (f32[1,4096]{1,0:T(1,128)S(1)}, f32[1,4096]{1,0:T(1,128)}, u32[]{:S(2)}) copy-start(f32[1,4096]{1,0:T(1,128)} %pot_hbm.1) | copy-start | bytes 49156

commit v4 on v3

--- a/solution.py
+++ b/solution.py
@@ -164,8 +164,10 @@
                 xsend[k, j, p].start()
 
     def tile(slot, jl, jr):
-        a, b = panel[jl, 0], panel[jl, 1]
         for part in (0, 1):
+            if slot == 4 and part == 1:
+                jl, jr = jr, jl
+            a, b = panel[jl, 0], panel[jl, 1]
             if part == 0:
                 s = contract(a, panel[jr, 0]) + contract(b, panel[jr, 1])
             else:
@@ -214,21 +216,23 @@
             for p in (0, 1):
                 xsend[k, j, p].wait_recv()
     pair[4] = tile(4, 1, 2)
-    pair[1] = tile(1, 0, 1)
+    pair[2] = tile(2, 0, 2)
     settle(4)
-    cross = send(acc.at[4], acc.at[3], rs, rr, xdev[1])
-    cross.start()
-    settle(1)
-    start_ship(1)
-    pair[2] = tile(2, 0, 2)
-    pass_on(0)
+    cross = [send(acc.at[4, p], acc.at[3, p], rs.at[p], rr.at[p], xdev[1 + p]) for p in (0, 1)]
+    for cp in cross:
+        cp.start()
     settle(2)
     start_ship(2)
-    pass_on(1)
-    cross.wait_recv()
+    pair[1] = tile(1, 0, 1)
+    pass_on(0)
+    settle(1)
+    for cp in cross:
+        cp.wait_recv()
     start_ship(3)
+    start_ship(1)
     pass_on(2)
     pass_on(3)
+    pass_on(1)
 
     total = acc[flip(r, c)]
     for k in (0, 1):
@@ -236,7 +240,7 @@
         total = total + land[k]
     inter[...] = total * dvol
 
-    for cp in [edge, cross] + list(pair.values()) + list(zsend.values()) + list(xsend.values()):
+    for cp in [edge] + cross + list(pair.values()) + list(zsend.values()) + list(xsend.values()):
         if cp is not edge:
             cp.wait_send()
     for t in (0, 1, 2, 3):
@@ -273,7 +277,7 @@
             pltpu.VMEM((2, 2, half, rows), jnp.float32),
             pltpu.VMEM((4, 2, half, rows), jnp.float32),
             dma((2,)), dma, dma, dma((2,)), dma((4, 2)), dma((4, 2)), dma((4, 3, 2)),
-            dma((4, 3, 2)), dma((5,)), dma((5,)), dma((4,)), dma((2,)), dma((4,)), dma, dma,
+            dma((4, 3, 2)), dma((5,)), dma((5,)), dma((4,)), dma((2,)), dma((4,)), dma((2,)), dma((2,)),
         ],
         compiler_params=pltpu.CompilerParams(
             collective_id=0, has_side_effects=True, vmem_limit_bytes=24000000

time: 66.8 us -> 65.8 us (0.985)
  the two profiles are of different devices: /device:TPU:7 before, /device:TPU:2 now
where the time goes in v4:
time: 65.8 us; the launch traced here: 65.6 us
  Pallas kernels  61.1 us (93%)
  local copies, waits for them, and re-layouts  3.81 us (6%)
    pallas_call x1, Pallas kernels, exchange(): pl.pallas_call(functools.partial(kernel, dvol), out_shape=(jax.ShapeDtype...  61.1 us
    unnamed x6, local copies, waits for them, and re-layouts  3.81 us

profile of v4, /device:TPU:2, one launch (start us, length us, event | category | flops | bytes accessed | tf_op | source)
XLA Modules:
  0.0 65.6 jit_solution(17803885470047366044)
XLA Ops:
  0.6 0.0 copy-start
  0.6 1.2 %copy-done = bf16[2,64,1,4096]{3,1,2,0:T(8,128)(2,1)S(1)} copy-done((bf16[2,64,1,4096]{3,1,2,0:T(8,128)(2,1)S(1)}, bf16[2,64,1,4096]{3,1,2,0:T(8,128)(2,1)}, u32[]{:S(2)}) %copy-start) | copy-done | bytes 1048600
  1.9 0.0 copy-start.1
  1.9 0.7 %copy-done.1 = f32[1,4096]{1,0:T(1,128)S(1)} copy-done((f32[1,4096]{1,0:T(1,128)S(1)}, f32[1,4096]{1,0:T(1,128)}, u32[]{:S(2)}) %copy-start.1) | copy-done | bytes 16408
  2.6 61.1 %overlap.1 = (f32[2,128,256]{2,1,0:T(8,128)S(1)}, bf16[2,64,4096]{2,1,0:T(8,128)(2,1)S(1)}) custom-call(bf16[2,64,4096]{2,1,0:T(8,128)(2,1)S(1)} %bitcast.5, f32[1,4096]{1,0:T(1,128)S(1)} %copy-done.1), custom_call_target="tpu_custom_call" | custom-call | tf_op jit(solution)/shard_map/overlap/pallas_call | solution.py:261
  63.7 0.9 %copy.4 = f32[128,2,256]{2,1,0:T(2,128)} copy(f32[128,2,256]{2,0,1:T(8,128)S(1)} %bitcast.7) | data formatting | bytes 524288
  64.6 1.0 %copy.7 = bf16[2,64,1,4096]{3,1,2,0:T(8,128)(2,1)} copy(bf16[2,64,1,4096]{3,1,2,0:T(8,128)(2,1)S(1)} %bitcast.6) | data formatting | bytes 2097152
Async XLA Ops:
  0.6 1.2 %copy-start = (bf16[2,64,1,4096]{3,1,2,0:T(8,128)(2,1)S(1)}, bf16[2,64,1,4096]{3,1,2,0:T(8,128)(2,1)}, u32[]{:S(2)}) copy-start(bf16[2,64,1,4096]{3,1,2,0:T(8,128)(2,1)} %param.2) | copy-start | bytes 3145732
  1.9 0.7 %copy-start.1 = (f32[1,4096]{1,0:T(1,128)S(1)}, f32[1,4096]{1,0:T(1,128)}, u32[]{:S(2)}) copy-start(f32[1,4096]{1,0:T(1,128)} %pot_hbm.1) | copy-start | bytes 49156
